TPU v7x, 32 devices: a whole 2x2x4 slice. The times are simulated.
32 devices in a mesh: row: 4 (over x, core), col: 8 (over z, y).
Axes of the slice: x: 2, y: 2, z: 4, core: 2. Of those that a mesh axis runs over, the one named last changes fastest.
Arguments:
- ancestor_inverse: bfloat16 [24576, 24576], P('row', 'col'), may hold values from -0.0390625 to 0.0390625
- panels: bfloat16 [24576, 3, 512], P(('row', 'col')), may hold values from -1.1953125 to 1.1953125
- diag_inverse: float32 [3, 512, 512], replicated, may hold values from -6 to 6
- tile_mask: int32 [3, 192], replicated, may hold values 0 or 1
Outputs:
- off_diagonal: float32 [24576, 3, 512], P(('row', 'col'))
- diagonal: float32 [3, 512, 512], replicated
All inputs are finite; a program needn't handle non-finite values.
Results may differ from a plain program's by a relative error of at most 0.0003.
Values may be sent and summed in bfloat16 or wider, within the bound.
A program may use at most 192 MiB of HBM per device.

v0:
```python
import jax
import jax.numpy as jnp
from jax import lax
from jax.sharding import PartitionSpec as P


def exchange(partial, axis):
    count = lax.axis_size(axis)
    rows, width = partial.shape
    return lax.psum_scatter(partial, axis, scatter_dimension=0, tiled=True)


def body(ancestor_inverse, panels, diag_inverse, tile_mask):
    row_count = lax.axis_size("row")
    col_count = lax.axis_size("col")
    span = lax.axis_index("row") * col_count + lax.axis_index("col")
    kept_rows = panels.shape[0]
    panel_count = panels.shape[1]
    tile = kept_rows * row_count * col_count // tile_mask.shape[1]
    full_mask = jnp.repeat(tile_mask, tile, axis=1).astype(jnp.bfloat16)
    own_mask = lax.dynamic_slice_in_dim(full_mask, span * kept_rows, kept_rows, 1)
    moves = [
        (index, index % row_count * col_count + index // row_count)
        for index in range(row_count * col_count)
    ]
    masked = [panels[:, p, :] * own_mask[p][:, None] for p in range(panel_count)]
    sent = [lax.ppermute(block, ("row", "col"), moves) for block in masked]
    sides = [lax.all_gather(block, "row", axis=0, tiled=True) for block in sent]
    results, parts = ([], [])
    for p in range(panel_count):
        partial = jnp.dot(ancestor_inverse, sides[p], preferred_element_type=jnp.float32)
        summed = -exchange(partial, "col")
        results.append(summed)
        parts.append(
            lax.dot_general(
                masked[p].astype(jnp.float32),
                summed,
                (((0,), (0,)), ((), ())),
                precision=lax.Precision.HIGHEST,
            )
        )
    off_diagonal = jnp.stack(results, axis=1)
    schur = lax.psum(jnp.stack(parts), ("row", "col"))
    return (off_diagonal, diag_inverse - schur)


def solution(mesh):
    return jax.shard_map(
        body,
        mesh=mesh,
        in_specs=(P("row", "col"), P(("row", "col"), None, None), P(), P()),
        out_specs=(P(("row", "col"), None, None), P()),
        check_vma=False,
    )
```

profile of v0, /device:TPU:0, one launch (start us, length us, event | category | flops | bytes accessed | tf_op | source)
XLA Modules:
  0.0 952.1 jit_solution(13903537531053839367)
XLA Ops:
  7.2 0.7 convert_element_type.10
  7.9 0.1 broadcast_bitcast_fusion
  8.1 0.1 copy.9
  8.2 0.1 dynamic-slice_reduce_fusion.2
  8.3 2.0 bitcast_multiply_fusion.2
  10.3 1.6 collective-permute-start.2
  12.0 1.6 collective-permute-start
  13.6 1.5 collective-permute-start.1
  15.2 86.4 %all-gather.8.cloned.1.call-done = bf16[3072,512]{1,0:T(8,128)(2,1)} async-done(((bf16[768,512]{1,0:T(8,128)(2,1)}), bf16[3072,512]{1,0:T(8,128)(2,1)}) %all-gather.8.cloned.1.call-update) | async-done | bytes 3145744 | tf_op jit(solution)/shard_map/all_gather | solution.py:28
  101.6 27.8 %convolution_bitcast_fusion = f32[6144,512]{0,1:T(8,128)} fusion(bf16[3072,512]{1,0:T(8,128)(2,1)} %all-gather.8.cloned.1.call-done, bf16[6144,3072]{1,0:T(8,128)(2,1)} %param.4), kind=kOutput, calls=%fused_computation | convolution fusion | flops 19327352832 | bytes 53477376 | tf_op jit(solution)/shard_map/dot_general | solution.py:31
  129.4 0.2 reduce-scatter.4.cloned.1.call-start
  129.7 5.6 all-gather.4.cloned.1.call-done
  135.3 27.7 %convolution_bitcast_fusion.2 = f32[6144,512]{0,1:T(8,128)} fusion(bf16[3072,512]{1,0:T(8,128)(2,1)} %all-gather.4.cloned.1.call-done, bf16[6144,3072]{1,0:T(8,128)(2,1)} %param.4), kind=kOutput, calls=%fused_computation.2 | convolution fusion | flops 19327352832 | bytes 53477376 | tf_op jit(solution)/shard_map/dot_general | solution.py:31
  163.1 0.3 reduce-scatter.6.cloned.1.call-start
  163.3 3.3 all-gather.6.cloned.1.call-done
  166.6 27.7 %convolution_bitcast_fusion.1 = f32[6144,512]{0,1:T(8,128)} fusion(bf16[3072,512]{1,0:T(8,128)(2,1)} %all-gather.6.cloned.1.call-done, bf16[6144,3072]{1,0:T(8,128)(2,1)} %param.4), kind=kOutput, calls=%fused_computation.1 | convolution fusion | flops 19327352832 | bytes 53477376 | tf_op jit(solution)/shard_map/dot_general | solution.py:31
  194.3 0.3 all-reduce.2.cloned.1.call-start
  194.6 182.9 %reduce-scatter.8.cloned.1.call-done = f32[768,512]{0,1:T(8,128)} async-done(((f32[6144,512]{0,1:T(8,128)}), f32[768,512]{0,1:T(8,128)}) %reduce-scatter.8.cloned.1.call-update) | async-done | bytes 1572880 | tf_op jit(solution)/shard_map/reduce_scatter | solution.py:10
  377.5 3.1 fusion.12
  380.7 206.9 %reduce-scatter.4.cloned.1.call-done = f32[768,512]{0,1:T(8,128)} async-done(((f32[6144,512]{0,1:T(8,128)}), f32[768,512]{0,1:T(8,128)}) %reduce-scatter.4.cloned.1.call-update) | async-done | bytes 1572880 | tf_op jit(solution)/shard_map/reduce_scatter | solution.py:10
  587.6 3.4 fusion.6
  590.9 206.7 %reduce-scatter.6.cloned.1.call-done = f32[768,512]{0,1:T(8,128)} async-done(((f32[6144,512]{0,1:T(8,128)}), f32[768,512]{0,1:T(8,128)}) %reduce-scatter.6.cloned.1.call-update) | async-done | bytes 1572880 | tf_op jit(solution)/shard_map/reduce_scatter | solution.py:10
  797.6 3.1 fusion.9
  800.7 2.0 pad_maximum_fusion.1
  802.7 1.4 copy-done
  804.1 0.1 negate_bitcast_fusion
  804.2 0.4 copy-done.2
  804.7 0.9 copy-done.1
  805.8 2.4 pad_maximum_fusion
  808.2 6.2 copy.6
  814.4 126.5 %all-reduce.2.cloned.1.call-done = f32[3,512,512]{2,1,0:T(8,128)} async-done(((f32[3,512,512]{2,1,0:T(8,128)}), f32[3,512,512]{2,1,0:T(8,128)}) %all-reduce.2.cloned.1.call-update) | async-done | bytes 3145744 | tf_op jit(solution)/shard_map/psum | solution.py:43
  941.0 4.3 sub.3
  (23 shorter events, 0.5 us)
Async XLA Ops:
  7.2 94.5 %all-gather.8.cloned.1.call-start = ((), (), s32[]{:S(2)}) async-start(), calls=%async_computation.7 | async-start | bytes 3932160 | tf_op jit(solution)/shard_map/all_gather | solution.py:28
  10.3 119.1 %copy-start.4 = (bf16[768,512]{1,0:T(8,128)(2,1)}, bf16[768,512]{1,0:T(8,128)(2,1)S(1)}, u32[]{:S(2)}) copy-start(bf16[768,512]{1,0:T(8,128)(2,1)S(1)} %get-tuple-element.7) | copy-start | bytes 2359300
  10.3 1.6 collective-permute-start.2
  11.9 123.4 %all-gather.4.cloned.1.call-start = ((), (), s32[]{:S(2)}) async-start(), calls=%async_computation.3 | async-start | bytes 3932160 | tf_op jit(solution)/shard_map/all_gather | solution.py:28
  12.0 1.6 collective-permute-start
  13.6 153.1 %all-gather.6.cloned.1.call-start = ((), (), s32[]{:S(2)}) async-start(), calls=%async_computation.5 | async-start | bytes 3932160 | tf_op jit(solution)/shard_map/all_gather | solution.py:28
  13.6 1.5 collective-permute-start.1
  15.2 362.4 %reduce-scatter.8.cloned.1.call-start = ((), (), s32[]{:S(2)}) async-start(), calls=%async_computation.8 | async-start | bytes 14155776 | tf_op jit(solution)/shard_map/reduce_scatter | solution.py:10
  129.4 458.1 %reduce-scatter.4.cloned.1.call-start = ((), (), s32[]{:S(2)}) async-start(), calls=%async_computation.4 | async-start | bytes 14155776 | tf_op jit(solution)/shard_map/reduce_scatter | solution.py:10
  163.1 634.6 %reduce-scatter.6.cloned.1.call-start = ((), (), s32[]{:S(2)}) async-start(), calls=%async_computation.6 | async-start | bytes 14155776 | tf_op jit(solution)/shard_map/reduce_scatter | solution.py:10
  194.3 746.7 %all-reduce.2.cloned.1.call-start = ((), (), s32[]{:S(2)}) async-start(), calls=%async_computation.9 | async-start | bytes 6291456 | tf_op jit(solution)/shard_map/psum | solution.py:43
  802.7 1.4 copy-start
  802.7 1.9 copy-start.2
  804.1 1.5 copy-start.1
  808.2 132.8 %copy-start.3 = (f32[3,512,512]{2,1,0:T(8,128)S(1)}, f32[3,512,512]{2,1,0:T(8,128)}, u32[]{:S(2)}) copy-start(f32[3,512,512]{2,1,0:T(8,128)} %param.6) | copy-start | bytes 9437188
Sparse Core Ops, SparseCore 0:
  12.0 89.5 all-gather.7
  103.2 32.0 all-gather.3
  136.9 29.7 all-gather.5
  170.0 207.4 reduce-scatter.7
  381.0 206.5 reduce-scatter.3
  591.0 206.5 reduce-scatter.5
  803.7 137.2 all-reduce.1
where the time goes:
time: 953 us; the launch traced here: 952 us
  waiting for transfers between devices  818 us (86%)
  matrix products  92.8 us (10%)
  between operations  14.2 us (1%)
  other arithmetic  11.7 us (1%)
    reduce_scatter x3, waiting for transfers between devices, exchange(): return lax.psum_scatter(partial, axis, scatter_dimension=0, tiled=True)  597 us
    psum x1, waiting for transfers between devices, body(): schur = lax.psum(jnp.stack(parts), ('row', 'col'))  127 us
    all_gather x3, waiting for transfers between devices, body(): sides = [lax.all_gather(block, 'row', axis=0, tiled=True) for block in sent]  95.3 us
    dot_general x3, matrix products, body(): jnp.dot(ancestor_inverse, sides[p], preferred_element_type=jnp.float32)  83.2 us
  transfers between devices with their start and end apart: 10, of which 7 were waited for; matrix products, arithmetic and copies ran while one was open for 10% of the time, Pallas kernels for 0%

commit v1 on v0

--- a/solution.py
+++ b/solution.py
@@ -40,7 +40,9 @@
             )
         )
     off_diagonal = jnp.stack(results, axis=1)
-    schur = lax.psum(jnp.stack(parts), ("row", "col"))
+    schur = jnp.stack(parts)
+    for name in ("col", "row"):
+        schur = lax.psum(schur, name)
     return (off_diagonal, diag_inverse - schur)
 
 

time: 953 us -> 1010 us (1.060)
  waiting for transfers between devices: 818 us -> 879 us
    psum x1 -> x2, waiting for transfers between devices: 127 us -> 187 us  [body(): schur = lax.psum(schur, name)]
  transfers between devices with their start and end apart: 10 -> 11, of which waited for: 7 -> 8; matrix products, arithmetic and copies ran while one was open for 10% -> 10% of each run, Pallas kernels for 0% -> 0%
where the time goes in v1:
time: 1010 us
  waiting for transfers between devices  879 us (87%)
  matrix products  92.8 us (9%)
  between operations  14.2 us (1%)
  other arithmetic  11.7 us (1%)
    reduce_scatter x3, waiting for transfers between devices, exchange(): return lax.psum_scatter(partial, axis, scatter_dimension=0, tiled=True)  597 us
    psum x2, waiting for transfers between devices, body(): schur = lax.psum(schur, name)  187 us
    all_gather x3, waiting for transfers between devices, body(): sides = [lax.all_gather(block, 'row', axis=0, tiled=True) for block in sent]  95.3 us
    dot_general x3, matrix products, body(): jnp.dot(ancestor_inverse, sides[p], preferred_element_type=jnp.float32)  83.2 us
  transfers between devices with their start and end apart: 11, of which 8 were waited for; matrix products, arithmetic and copies ran while one was open for 10% of the time, Pallas kernels for 0%

profile of v1, /device:TPU:0, one launch (start us, length us, event | category | flops | bytes accessed | tf_op | source)
XLA Modules:
  0.0 1011.8 jit_solution(8316045815498323731)
XLA Ops:
  7.2 0.7 convert_element_type.10
  7.9 0.1 broadcast_bitcast_fusion
  8.1 0.1 copy.9
  8.2 0.1 dynamic-slice_reduce_fusion.2
  8.3 2.0 bitcast_multiply_fusion.2
  10.3 1.6 collective-permute-start.2
  12.0 1.6 collective-permute-start
  13.6 1.5 collective-permute-start.1
  15.2 86.4 %all-gather.8.cloned.1.call-done = bf16[3072,512]{1,0:T(8,128)(2,1)} async-done(((bf16[768,512]{1,0:T(8,128)(2,1)}), bf16[3072,512]{1,0:T(8,128)(2,1)}) %all-gather.8.cloned.1.call-update) | async-done | bytes 3145744 | tf_op jit(solution)/shard_map/all_gather | solution.py:28
  101.6 27.8 %convolution_bitcast_fusion = f32[6144,512]{0,1:T(8,128)} fusion(bf16[3072,512]{1,0:T(8,128)(2,1)} %all-gather.8.cloned.1.call-done, bf16[6144,3072]{1,0:T(8,128)(2,1)} %param.4), kind=kOutput, calls=%fused_computation | convolution fusion | flops 19327352832 | bytes 53477376 | tf_op jit(solution)/shard_map/dot_general | solution.py:31
  129.4 0.2 reduce-scatter.4.cloned.1.call-start
  129.7 5.6 all-gather.4.cloned.1.call-done
  135.3 27.7 %convolution_bitcast_fusion.2 = f32[6144,512]{0,1:T(8,128)} fusion(bf16[3072,512]{1,0:T(8,128)(2,1)} %all-gather.4.cloned.1.call-done, bf16[6144,3072]{1,0:T(8,128)(2,1)} %param.4), kind=kOutput, calls=%fused_computation.2 | convolution fusion | flops 19327352832 | bytes 53477376 | tf_op jit(solution)/shard_map/dot_general | solution.py:31
  163.1 0.3 reduce-scatter.6.cloned.1.call-start
  163.3 3.3 all-gather.6.cloned.1.call-done
  166.6 27.7 %convolution_bitcast_fusion.1 = f32[6144,512]{0,1:T(8,128)} fusion(bf16[3072,512]{1,0:T(8,128)(2,1)} %all-gather.6.cloned.1.call-done, bf16[6144,3072]{1,0:T(8,128)(2,1)} %param.4), kind=kOutput, calls=%fused_computation.1 | convolution fusion | flops 19327352832 | bytes 53477376 | tf_op jit(solution)/shard_map/dot_general | solution.py:31
  194.3 0.3 all-reduce.3.cloned.1.call-start
  194.6 182.9 %reduce-scatter.8.cloned.1.call-done = f32[768,512]{0,1:T(8,128)} async-done(((f32[6144,512]{0,1:T(8,128)}), f32[768,512]{0,1:T(8,128)}) %reduce-scatter.8.cloned.1.call-update) | async-done | bytes 1572880 | tf_op jit(solution)/shard_map/reduce_scatter | solution.py:10
  377.5 3.1 fusion.12
  380.7 206.9 %reduce-scatter.4.cloned.1.call-done = f32[768,512]{0,1:T(8,128)} async-done(((f32[6144,512]{0,1:T(8,128)}), f32[768,512]{0,1:T(8,128)}) %reduce-scatter.4.cloned.1.call-update) | async-done | bytes 1572880 | tf_op jit(solution)/shard_map/reduce_scatter | solution.py:10
  587.6 3.4 fusion.6
  590.9 206.7 %reduce-scatter.6.cloned.1.call-done = f32[768,512]{0,1:T(8,128)} async-done(((f32[6144,512]{0,1:T(8,128)}), f32[768,512]{0,1:T(8,128)}) %reduce-scatter.6.cloned.1.call-update) | async-done | bytes 1572880 | tf_op jit(solution)/shard_map/reduce_scatter | solution.py:10
  797.6 3.1 fusion.9
  800.7 2.0 pad_maximum_fusion.1
  802.8 127.9 %all-reduce.3.cloned.1.call-done = f32[3,512,512]{2,1,0:T(8,128)} async-done(((f32[3,512,512]{2,1,0:T(8,128)}), f32[3,512,512]{2,1,0:T(8,128)}) %all-reduce.3.cloned.1.call-update) | async-done | bytes 3145744 | tf_op jit(solution)/shard_map/psum | solution.py:45
  930.8 0.1 negate_bitcast_fusion
  930.9 1.2 copy-done.2
  932.2 0.4 copy-done.1
  932.7 2.4 pad_maximum_fusion
  935.2 6.4 copy.6
  941.6 59.0 %all-reduce.5.cloned.1.call-done = f32[3,512,512]{2,1,0:T(8,128)} async-done(((f32[3,512,512]{2,1,0:T(8,128)}), f32[3,512,512]{2,1,0:T(8,128)}) %all-reduce.5.cloned.1.call-update) | async-done | bytes 3145744 | tf_op jit(solution)/shard_map/psum | solution.py:45
  1000.6 4.3 sub.3
  (26 shorter events, 0.6 us)
Async XLA Ops:
  7.2 94.5 %all-gather.8.cloned.1.call-start = ((), (), s32[]{:S(2)}) async-start(), calls=%async_computation.7 | async-start | bytes 3932160 | tf_op jit(solution)/shard_map/all_gather | solution.py:28
  10.3 119.1 %copy-start.4 = (bf16[768,512]{1,0:T(8,128)(2,1)}, bf16[768,512]{1,0:T(8,128)(2,1)S(1)}, u32[]{:S(2)}) copy-start(bf16[768,512]{1,0:T(8,128)(2,1)S(1)} %get-tuple-element.7) | copy-start | bytes 2359300
  10.3 1.6 collective-permute-start.2
  11.9 123.4 %all-gather.4.cloned.1.call-start = ((), (), s32[]{:S(2)}) async-start(), calls=%async_computation.3 | async-start | bytes 3932160 | tf_op jit(solution)/shard_map/all_gather | solution.py:28
  12.0 1.6 collective-permute-start
  13.6 153.1 %all-gather.6.cloned.1.call-start = ((), (), s32[]{:S(2)}) async-start(), calls=%async_computation.5 | async-start | bytes 3932160 | tf_op jit(solution)/shard_map/all_gather | solution.py:28
  13.6 1.5 collective-permute-start.1
  15.2 362.4 %reduce-scatter.8.cloned.1.call-start = ((), (), s32[]{:S(2)}) async-start(), calls=%async_computation.8 | async-start | bytes 14155776 | tf_op jit(solution)/shard_map/reduce_scatter | solution.py:10
  129.4 458.1 %reduce-scatter.4.cloned.1.call-start = ((), (), s32[]{:S(2)}) async-start(), calls=%async_computation.4 | async-start | bytes 14155776 | tf_op jit(solution)/shard_map/reduce_scatter | solution.py:10
  163.1 634.6 %reduce-scatter.6.cloned.1.call-start = ((), (), s32[]{:S(2)}) async-start(), calls=%async_computation.6 | async-start | bytes 14155776 | tf_op jit(solution)/shard_map/reduce_scatter | solution.py:10
  194.3 736.4 %all-reduce.3.cloned.1.call-start = ((), (), s32[]{:S(2)}) async-start(), calls=%async_computation.9 | async-start | bytes 6291456 | tf_op jit(solution)/shard_map/psum | solution.py:45
  802.7 128.0 %copy-start = (f32[768,512]{0,1:T(8,128)S(1)}, f32[768,512]{0,1:T(8,128)}, u32[]{:S(2)}) copy-start(f32[768,512]{0,1:T(8,128)} %reduce-scatter.8.cloned.1.call-done) | copy-start | bytes 4718596
  802.7 197.9 %all-reduce.5.cloned.1.call-start = ((), (), s32[]{:S(2)}) async-start(), calls=%async_computation.10 | async-start | bytes 6291456 | tf_op jit(solution)/shard_map/psum | solution.py:45
  930.7 1.4 copy-start.2
  930.8 1.9 copy-start.1
  935.2 65.4 %copy-start.3 = (f32[3,512,512]{2,1,0:T(8,128)S(1)}, f32[3,512,512]{2,1,0:T(8,128)}, u32[]{:S(2)}) copy-start(f32[3,512,512]{2,1,0:T(8,128)} %param.6) | copy-start | bytes 9437188
Sparse Core Ops, SparseCore 0:
  12.0 89.5 all-gather.7
  103.2 32.0 all-gather.3
  136.9 29.7 all-gather.5
  170.0 207.4 reduce-scatter.7
  381.0 206.5 reduce-scatter.3
  591.0 206.5 reduce-scatter.5
  802.9 127.8 all-reduce.2
  933.1 67.4 all-reduce.4
